TPU v7x, 256 devices: a whole 4x4x8 slice. The times are simulated.
256 devices in a mesh: tm: 64 (over z, x, core), blk: 4 (over y).
Axes of the slice: x: 4, y: 4, z: 8, core: 2. Of those that a mesh axis runs over, the one named last changes fastest.
Arguments:
- prior_mean: float32 [512], replicated, may hold values from -6 to 6
- after_mean: float32 [512], replicated, may hold values from -6 to 6
- filter_map: float32 [128, 512, 512], P('tm', 'blk'), may hold values from -1 to 1.5
- smoother_gain: float32 [128, 512, 512], P('tm', 'blk'), may hold values from -1 to 1.5
- smoother_map: float32 [128, 512, 512], P('tm', 'blk'), may hold values from -1 to 1.5
- obs_gain: float32 [128, 512, 128], P('tm', 'blk'), may hold values from -0.5 to 0.5
- observations: float32 [128, 128], P('tm'), may hold values from -6 to 6
Outputs:
- filtered: float32 [128, 512], P('tm', 'blk')
- smoothed: float32 [128, 512], P('tm', 'blk')
All inputs are finite; a program needn't handle non-finite values.
Results may differ from a plain program's by a relative error of at most 0.0003.
Values sent between devices are 32-bit elements; how exact they have to be, the bound alone decides.
A program may use at most 128 MiB of HBM per device.

v0:
```python
import jax
import jax.numpy as jnp
from jax import lax
from jax.sharding import Mesh
from jax.sharding import PartitionSpec as P

TM = ("tm_0", "tm_1", "tm_2")


def neutral_like(value, identity):
    return jax.tree.map(
        lambda part, zero: jnp.zeros_like(part) + jnp.asarray(zero, part.dtype), value, identity
    )


def prefix_by_axis(value, axes, combine, identity, reverse):
    before = start = neutral_like(value, identity)
    so_far = value
    for axis in reversed(axes):
        length, index = (lax.axis_size(axis), lax.axis_index(axis))
        pieces = jax.tree.map(lambda part: lax.all_gather(part, axis), so_far)
        inside, so_far = (start, start)
        for k in reversed(range(length)) if reverse else range(length):
            passed = k > index if reverse else k < index
            so_far = combine(so_far, jax.tree.map(lambda part: part[k], pieces))
            inside = jax.tree.map(lambda new, old: jnp.where(passed, new, old), so_far, inside)
        before = combine(inside, before)
    return before


def chain_combine(earlier, later):
    highest = lax.Precision.HIGHEST
    joined_map = jnp.dot(later[0], earlier[0], precision=highest)
    joined_offset = jnp.dot(later[0], earlier[1], precision=highest) + later[1]
    return (joined_map, joined_offset)


def shards(prior_mean, after_mean, filter_map, smoother_gain, smoother_map, obs_gain, observations):
    highest = lax.Precision.HIGHEST
    steps = filter_map.shape[0]
    rows = filter_map.shape[1]
    width = filter_map.shape[2]
    first_row = lax.axis_index("blk") * rows
    drive_rows = jnp.einsum("tro,to->tr", obs_gain, observations, precision=highest)
    full_filter, full_gain, drive = (
        lax.all_gather(filter_map, "blk", axis=1, tiled=True),
        lax.all_gather(smoother_gain, "blk", axis=1, tiled=True),
        lax.all_gather(drive_rows, "blk", axis=1, tiled=True),
    )
    identity = jnp.eye(width, dtype=jnp.float32)
    nothing = jnp.zeros((width,), jnp.float32)
    offset = nothing
    for index in range(steps):
        offset = jnp.dot(full_filter[index], offset, precision=highest) + drive[index]
    composite = full_filter[steps - 1]
    index = 0
    composite = jnp.dot(composite, full_filter[index], precision=highest)
    total = prefix_by_axis((composite, offset), TM, chain_combine, (identity, nothing), False)
    entering = jnp.dot(total[0], prior_mean, precision=highest) + total[1]
    current = entering
    filtered_list = []
    for index in range(steps):
        current = jnp.dot(full_filter[index], current, precision=highest) + drive[index]
        filtered_list.append(current)
    filtered_full = jnp.stack(filtered_list, axis=0)
    filtered_rows = lax.dynamic_slice_in_dim(filtered_full, first_row, rows, 1)
    pulled_rows = jnp.einsum("trk,tk->tr", smoother_map, filtered_full, precision=highest)
    pulled = lax.all_gather(pulled_rows, "blk", axis=1, tiled=True)
    offset = nothing
    for index in range(steps - 1, -1, -1):
        offset = jnp.dot(full_gain[index], offset, precision=highest) + pulled[index]
    composite = full_gain[0]
    index = 1
    composite = jnp.dot(composite, full_gain[index], precision=highest)
    total = prefix_by_axis((composite, offset), TM, chain_combine, (identity, nothing), True)
    leaving = jnp.dot(total[0], after_mean, precision=highest) + total[1]
    current = leaving
    smoothed_list = []
    for index in range(steps - 1, -1, -1):
        current = jnp.dot(full_gain[index], current, precision=highest) + pulled[index]
        smoothed_list.append(current)
    smoothed_full = jnp.stack(smoothed_list[::-1], axis=0)
    smoothed_rows = lax.dynamic_slice_in_dim(smoothed_full, first_row, rows, 1)
    return (filtered_rows, smoothed_rows)


def solution(mesh):
    torus = Mesh(mesh.devices.reshape(8, 4, 2, mesh.shape["blk"]), ("tm_0", "tm_1", "tm_2", "blk"))
    in_specs = (
        P(),
        P(),
        P(TM, "blk", None),
        P(TM, "blk", None),
        P(TM, "blk", None),
        P(TM, "blk", None),
        P(TM, None),
    )
    out_specs = (P(TM, "blk"), P(TM, "blk"))
    return jax.shard_map(
        shards, mesh=torus, in_specs=in_specs, out_specs=out_specs, check_vma=False
    )
```

profile of v0, /device:TPU:1, one launch (start us, length us, event | category | flops | bytes accessed | tf_op | source)
XLA Modules:
  0.0 462.8 jit_solution(7283257458123513231)
XLA Ops:
  8.7 38.1 %all-gather.27.cloned.1.call-done = f32[2,512,512]{2,1,0:T(8,128)} async-done(((f32[2,128,512]{2,1,0:T(8,128)}), f32[2,512,512]{2,1,0:T(8,128)}) %all-gather.27.cloned.1.call-update) | async-done | bytes 2097168 | tf_op jit(solution)/shard_map/all_gather | solution.py:46
  46.8 4.4 fusion.142
  51.2 30.8 %all-gather.29.cloned.1.call-done = f32[2,512,512]{2,1,0:T(8,128)} async-done(((f32[2,128,512]{2,1,0:T(8,128)}), f32[2,512,512]{2,1,0:T(8,128)}) %all-gather.29.cloned.1.call-update) | async-done | bytes 2097168 | tf_op jit(solution)/shard_map/all_gather | solution.py:47
  82.0 4.4 fusion.147
  86.5 14.2 %all-gather.31.cloned.1.call-done = f32[1024,512]{1,0:T(8,128)} async-done(((f32[512,512]{1,0:T(8,128)}), f32[1024,512]{1,0:T(8,128)}) %all-gather.31.cloned.1.call-update) | async-done | bytes 2097168 | tf_op jit(solution)/shard_map/all_gather | solution.py:21
  102.9 4.4 fusion.136
  107.4 12.2 %all-gather.37.cloned.1.call-done = f32[1024,512]{1,0:T(8,128)} async-done(((f32[512,512]{1,0:T(8,128)}), f32[1024,512]{1,0:T(8,128)}) %all-gather.37.cloned.1.call-update) | async-done | bytes 2097168 | tf_op jit(solution)/shard_map/all_gather | solution.py:21
  121.8 4.4 fusion.84
  126.4 46.0 %all-gather.33.cloned.1.call-done = f32[2048,512]{1,0:T(8,128)} async-done(((f32[512,512]{1,0:T(8,128)}), f32[2048,512]{1,0:T(8,128)}) %all-gather.33.cloned.1.call-update) | async-done | bytes 4194320 | tf_op jit(solution)/shard_map/all_gather | solution.py:21
  175.8 3.1 fusion.121
  182.7 2.8 fusion.129
  186.0 8.1 %all_gather.91 = f32[2,512]{1,0:T(2,128)S(1)} all-gather(f32[2,128]{1,0:T(2,128)S(1)} %bitcast.347), channel_id=1, replica_groups=mesh['tm_0'=8,'tm_1'=4,'tm_2'=2,'blk'=4] {'blk'}, dimensions={1}, use_global_device_ids=true | all-gather | bytes 5120 | tf_op jit(solution)/shard_map/all_gather | solution.py:48
  198.5 4.2 all-gather.12
  203.6 21.6 %all-gather.39.cloned.1.call-done = f32[2048,512]{1,0:T(8,128)} async-done(((f32[512,512]{1,0:T(8,128)}), f32[2048,512]{1,0:T(8,128)}) %all-gather.39.cloned.1.call-update) | async-done | bytes 4194320 | tf_op jit(solution)/shard_map/all_gather | solution.py:21
  228.5 3.1 fusion.69
  235.5 2.8 fusion.77
  238.4 2.5 fusion.134
  243.2 9.4 %all-gather.13 = f32[4,1,512]{2,1,0:T(1,128)S(1)} all-gather(f32[1,1,512]{2,1,0:T(1,128)S(1)} %bitcast.331), channel_id=6, replica_groups=mesh['tm_0'=8,'tm_1'=4,'tm_2'=2,'blk'=4] {'tm_1'}, dimensions={0}, use_global_device_ids=true | all-gather | bytes 10240 | tf_op jit(solution)/shard_map/all_gather | solution.py:21
  261.7 22.3 %all-gather.14 = f32[8,1,512]{2,1,0:T(1,128)S(1)} all-gather(f32[1,1,512]{2,1,0:T(1,128)S(1)} %bitcast.342), channel_id=7, replica_groups=mesh['tm_0'=8,'tm_1'=4,'tm_2'=2,'blk'=4] {'tm_0'}, dimensions={0}, use_global_device_ids=true | all-gather | bytes 18432 | tf_op jit(solution)/shard_map/all_gather | solution.py:21
  284.0 2.4 fusion.67
  287.4 3.0 fusion.6
  290.4 3.0 fusion.20
  293.4 28.4 %all-gather.35.cloned.1.call-done = f32[4096,512]{1,0:T(8,128)} async-done(((f32[512,512]{1,0:T(8,128)}), f32[4096,512]{1,0:T(8,128)}) %all-gather.35.cloned.1.call-update) | async-done | bytes 8388624 | tf_op jit(solution)/shard_map/all_gather | solution.py:21
  324.1 2.3 fusion.93
  326.5 2.5 fusion.97
  361.3 8.5 %all_gather.105 = f32[2,512]{1,0:T(2,128)S(1)} all-gather(f32[2,128]{1,0:T(2,128)S(1)} %bitcast.346), channel_id=1, replica_groups=mesh['tm_0'=8,'tm_1'=4,'tm_2'=2,'blk'=4] {'blk'}, dimensions={1}, use_global_device_ids=true | all-gather | bytes 5120 | tf_op jit(solution)/shard_map/all_gather | solution.py:68
  370.8 3.6 all-gather.15
  375.4 9.5 %all-gather.16 = f32[4,1,512]{2,1,0:T(1,128)S(1)} all-gather(f32[1,1,512]{2,1,0:T(1,128)S(1)} %bitcast.330), channel_id=12, replica_groups=mesh['tm_0'=8,'tm_1'=4,'tm_2'=2,'blk'=4] {'tm_1'}, dimensions={0}, use_global_device_ids=true | all-gather | bytes 10240 | tf_op jit(solution)/shard_map/all_gather | solution.py:21
  387.9 19.5 %all-gather.17 = f32[8,1,512]{2,1,0:T(1,128)S(1)} all-gather(f32[1,1,512]{2,1,0:T(1,128)S(1)} %bitcast.339), channel_id=13, replica_groups=mesh['tm_0'=8,'tm_1'=4,'tm_2'=2,'blk'=4] {'tm_0'}, dimensions={0}, use_global_device_ids=true | all-gather | bytes 18432 | tf_op jit(solution)/shard_map/all_gather | solution.py:21
  408.7 7.8 %all-gather.41.cloned.1.call-done = f32[4096,512]{1,0:T(8,128)} async-done(((f32[512,512]{1,0:T(8,128)}), f32[4096,512]{1,0:T(8,128)}) %all-gather.41.cloned.1.call-update) | async-done | bytes 8388624 | tf_op jit(solution)/shard_map/all_gather | solution.py:21
  418.8 2.3 fusion.41
  421.2 2.5 fusion.45
  (206 shorter events, 113.7 us)
Async XLA Ops:
  7.2 353.7 %copy-start = (f32[2,128,512]{2,1,0:T(8,128)S(1)}, f32[2,128,512]{2,1,0:T(8,128)}, u32[]{:S(2)}) copy-start(f32[2,128,512]{2,1,0:T(8,128)} %param.11) | copy-start | bytes 1572868
  7.2 39.6 %all-gather.27.cloned.1.call-start = ((), (), s32[]{:S(2)}) async-start(), calls=%async_computation | async-start | bytes 2621440 | tf_op jit(solution)/shard_map/all_gather | solution.py:46
  7.9 74.1 %all-gather.29.cloned.1.call-start = ((), (), s32[]{:S(2)}) async-start(), calls=%async_computation.1 | async-start | bytes 2621440 | tf_op jit(solution)/shard_map/all_gather | solution.py:47
  8.7 92.0 %all-gather.31.cloned.1.call-start = ((), (), s32[]{:S(2)}) async-start(), calls=%async_computation.2 | async-start | bytes 3145728 | tf_op jit(solution)/shard_map/all_gather | solution.py:21
  51.2 68.4 %all-gather.37.cloned.1.call-start = ((), (), s32[]{:S(2)}) async-start(), calls=%async_computation.5 | async-start | bytes 3145728 | tf_op jit(solution)/shard_map/all_gather | solution.py:21
  86.4 86.0 %all-gather.33.cloned.1.call-start = ((), (), s32[]{:S(2)}) async-start(), calls=%async_computation.3 | async-start | bytes 5242880 | tf_op jit(solution)/shard_map/all_gather | solution.py:21
  102.9 23.3 %copy-start.13 = (f32[512,512]{1,0:T(8,128)}, f32[512,512]{1,0:T(8,128)S(1)}, u32[]{:S(2)}) copy-start(f32[512,512]{1,0:T(8,128)S(1)} %fusion.35) | copy-start | bytes 3145732
  107.3 117.9 %all-gather.39.cloned.1.call-start = ((), (), s32[]{:S(2)}) async-start(), calls=%async_computation.6 | async-start | bytes 5242880 | tf_op jit(solution)/shard_map/all_gather | solution.py:21
  121.8 53.0 %copy-start.16 = (f32[512,512]{1,0:T(8,128)}, f32[512,512]{1,0:T(8,128)S(1)}, u32[]{:S(2)}) copy-start(f32[512,512]{1,0:T(8,128)S(1)} %fusion.31) | copy-start | bytes 3145732
  126.2 195.6 %all-gather.35.cloned.1.call-start = ((), (), s32[]{:S(2)}) async-start(), calls=%async_computation.4 | async-start | bytes 9437184 | tf_op jit(solution)/shard_map/all_gather | solution.py:21
  172.4 7.4 %copy-start.7 = (f32[2048,512]{1,0:T(8,128)S(1)}, f32[2048,512]{1,0:T(8,128)}, u32[]{:S(2)}) copy-start(f32[2048,512]{1,0:T(8,128)} %all-gather.33.cloned.1.call-done) | copy-start | bytes 12582916
  179.8 22.9 %copy-start.3 = (f32[2,512,512]{2,1,0:T(8,128)S(1)}, f32[2,512,512]{2,1,0:T(8,128)}, u32[]{:S(2)}) copy-start(f32[2,512,512]{2,1,0:T(8,128)} %all-gather.29.cloned.1.call-done) | copy-start | bytes 6291460
  185.6 231.0 %all-gather.41.cloned.1.call-start = ((), (), s32[]{:S(2)}) async-start(), calls=%async_computation.7 | async-start | bytes 9437184 | tf_op jit(solution)/shard_map/all_gather | solution.py:21
  225.2 7.4 %copy-start.5 = (f32[2048,512]{1,0:T(8,128)S(1)}, f32[2048,512]{1,0:T(8,128)}, u32[]{:S(2)}) copy-start(f32[2048,512]{1,0:T(8,128)} %all-gather.39.cloned.1.call-done) | copy-start | bytes 12582916
  238.3 16.9 %copy-start.14 = (f32[512,512]{1,0:T(8,128)S(1)}, f32[512,512]{1,0:T(8,128)}, u32[]{:S(2)}) copy-start(f32[512,512]{1,0:T(8,128)} %copy-done.13) | copy-start | bytes 3145732
  238.3 16.9 %copy-start.15 = (f32[512,512]{1,0:T(8,128)S(1)}, f32[512,512]{1,0:T(8,128)}, u32[]{:S(2)}) copy-start(f32[512,512]{1,0:T(8,128)} %fusion.136) | copy-start | bytes 3145732
  238.3 18.1 %copy-start.17 = (f32[512,512]{1,0:T(8,128)S(1)}, f32[512,512]{1,0:T(8,128)}, u32[]{:S(2)}) copy-start(f32[512,512]{1,0:T(8,128)} %copy-done.16) | copy-start | bytes 3145732
  238.3 18.1 %copy-start.18 = (f32[512,512]{1,0:T(8,128)S(1)}, f32[512,512]{1,0:T(8,128)}, u32[]{:S(2)}) copy-start(f32[512,512]{1,0:T(8,128)} %fusion.84) | copy-start | bytes 3145732
  240.8 16.8 %copy-start.8 = (f32[2048,512]{1,0:T(8,128)S(1)}, f32[2048,512]{1,0:T(8,128)}, u32[]{:S(2)}) copy-start(f32[2048,512]{1,0:T(8,128)} %all-gather.33.cloned.1.call-done) | copy-start | bytes 12582916
  256.4 31.0 %copy-start.10 = (f32[512,512]{1,0:T(8,128)S(1)}, f32[512,512]{1,0:T(8,128)}, u32[]{:S(2)}) copy-start(f32[512,512]{1,0:T(8,128)} %copy-done.9) | copy-start | bytes 3145732
  256.4 31.0 %copy-start.12 = (f32[512,512]{1,0:T(8,128)S(1)}, f32[512,512]{1,0:T(8,128)}, u32[]{:S(2)}) copy-start(f32[512,512]{1,0:T(8,128)} %copy-done.11) | copy-start | bytes 3145732
  256.4 31.0 %copy-start.25 = (f32[512,512]{1,0:T(8,128)S(1)}, f32[512,512]{1,0:T(8,128)}, u32[]{:S(2)}) copy-start(f32[512,512]{1,0:T(8,128)} %fusion.129) | copy-start | bytes 3145732
  256.4 31.0 %copy-start.27 = (f32[512,512]{1,0:T(8,128)S(1)}, f32[512,512]{1,0:T(8,128)}, u32[]{:S(2)}) copy-start(f32[512,512]{1,0:T(8,128)} %copy-done.26) | copy-start | bytes 3145732
  257.6 32.8 %copy-start.31 = (f32[512,512]{1,0:T(8,128)}, f32[512,512]{1,0:T(8,128)S(1)}, u32[]{:S(2)}) copy-start(f32[512,512]{1,0:T(8,128)S(1)} %fusion.15) | copy-start | bytes 3145732
  284.0 6.4 %copy-start.22 = (f32[512,512]{1,0:T(8,128)S(1)}, f32[512,512]{1,0:T(8,128)}, u32[]{:S(2)}) copy-start(f32[512,512]{1,0:T(8,128)} %copy-done.21) | copy-start | bytes 3145732
  321.8 18.5 %copy-start.30 = (f32[512,512]{1,0:T(8,128)S(1)}, f32[512,512]{1,0:T(8,128)}, u32[]{:S(2)}) copy-start(f32[512,512]{1,0:T(8,128)} %fusion.6) | copy-start | bytes 3145732
  324.1 17.1 %copy-start.2 = (f32[4096,512]{1,0:T(8,128)S(1)}, f32[4096,512]{1,0:T(8,128)}, u32[]{:S(2)}) copy-start(f32[4096,512]{1,0:T(8,128)} %all-gather.35.cloned.1.call-done) | copy-start | bytes 25165828
  353.6 20.8 %copy-start.33 = (f32[1024,512]{1,0:T(8,128)S(1)}, f32[1024,512]{1,0:T(8,128)}, u32[]{:S(2)}) copy-start(f32[1024,512]{1,0:T(8,128)} %all-gather.37.cloned.1.call-done) | copy-start | bytes 6291460
  355.9 28.9 %copy-start.6 = (f32[2048,512]{1,0:T(8,128)S(1)}, f32[2048,512]{1,0:T(8,128)}, u32[]{:S(2)}) copy-start(f32[2048,512]{1,0:T(8,128)} %all-gather.39.cloned.1.call-done) | copy-start | bytes 12582916
  358.8 48.9 %copy-start.32 = (f32[512,512]{1,0:T(8,128)S(1)}, f32[512,512]{1,0:T(8,128)}, u32[]{:S(2)}) copy-start(f32[512,512]{1,0:T(8,128)} %copy-done.31) | copy-start | bytes 3145732
  416.5 18.3 %copy-start.24 = (f32[512,512]{1,0:T(8,128)S(1)}, f32[512,512]{1,0:T(8,128)}, u32[]{:S(2)}) copy-start(f32[512,512]{1,0:T(8,128)} %fusion.20) | copy-start | bytes 3145732
  418.8 17.0 %copy-start.1 = (f32[4096,512]{1,0:T(8,128)S(1)}, f32[4096,512]{1,0:T(8,128)}, u32[]{:S(2)}) copy-start(f32[4096,512]{1,0:T(8,128)} %all-gather.41.cloned.1.call-done) | copy-start | bytes 25165828
  (14 other events, 48.1 us)
Sparse Core Ops, SparseCore 0:
  9.8 36.9 all-gather.26
  48.6 33.3 all-gather.28
  83.8 16.8 all-gather.30
  102.3 17.1 all-gather.36
  121.2 51.1 all-gather.32
  174.1 51.0 all-gather.38
  227.0 94.7 all-gather.34
  323.6 92.9 all-gather.40
where the time goes:
time: 471 us; the launch traced here: 463 us
  waiting for transfers between devices  200 us (42%)
  matrix products  155 us (33%)
  blocking collectives  85.1 us (18%)
  between operations  15.1 us (3%)
  local copies, waits for them, and re-layouts  6.15 us (1%)
    all_gather x6, waiting for transfers between devices, prefix_by_axis(): pieces = jax.tree.map(lambda part: lax.all_gather(part, axis), so_far)  130 us
    dot_general x34, matrix products, chain_combine(): joined_map = jnp.dot(later[0], earlier[0], precision=highest)  74.4 us
    all_gather x6, blocking collectives, prefix_by_axis(): pieces = jax.tree.map(lambda part: lax.all_gather(part, axis), so_far)  68.5 us
    dot_general x34, matrix products, chain_combine(): joined_offset = jnp.dot(later[0], earlier[1], precision=highest) + later[1]  58.5 us
    all_gather x1, waiting for transfers between devices, shards(): lax.all_gather(filter_map, 'blk', axis=1, tiled=True)  38.1 us
    all_gather x1, waiting for transfers between devices, shards(): lax.all_gather(smoother_gain, 'blk', axis=1, tiled=True)  30.8 us
  transfers between devices with their start and end apart: 8, of which 8 were waited for; matrix products, arithmetic and copies ran while one was open for 25% of the time, Pallas kernels for 0%

commit v1 on v0

--- a/solution.py
+++ b/solution.py
@@ -42,9 +42,17 @@
     width = filter_map.shape[2]
     first_row = lax.axis_index("blk") * rows
     drive_rows = jnp.einsum("tro,to->tr", obs_gain, observations, precision=highest)
+
+    def set_the_sites(buf):
+        samples = []
+        for _ in range(jax.lax.axis_size("blk")):
+            samples.append(buf)
+        formed = jnp.concatenate(jax.lax.all_to_all(jnp.stack(samples), "blk", 0, 0), axis=1)
+        return formed
+
     full_filter, full_gain, drive = (
         lax.all_gather(filter_map, "blk", axis=1, tiled=True),
-        lax.all_gather(smoother_gain, "blk", axis=1, tiled=True),
+        set_the_sites(smoother_gain),
         lax.all_gather(drive_rows, "blk", axis=1, tiled=True),
     )
     identity = jnp.eye(width, dtype=jnp.float32)

time: 471 us -> 517 us (1.098)
  the two profiles are of different devices: /device:TPU:1 before, /device:TPU:32 now
where the time goes in v1:
time: 517 us; the launch traced here: 509 us
  waiting for transfers between devices  194 us (38%)
  matrix products  152 us (29%)
  blocking collectives  135 us (26%)
  between operations  15.2 us (3%)
  local copies, waits for them, and re-layouts  10.8 us (2%)
    all_gather x6, waiting for transfers between devices, prefix_by_axis(): pieces = jax.tree.map(lambda part: lax.all_gather(part, axis), so_far)  193 us
    dot_general x34, matrix products, chain_combine(): joined_map = jnp.dot(later[0], earlier[0], precision=highest)  77.5 us
    all_gather x6, blocking collectives, prefix_by_axis(): pieces = jax.tree.map(lambda part: lax.all_gather(part, axis), so_far)  72.7 us
    dot_general x34, matrix products, chain_combine(): joined_offset = jnp.dot(later[0], earlier[1], precision=highest) + later[1]  55.6 us
    all_to_all x1, blocking collectives, set_the_sites(): jax.lax.all_to_all(jnp.stack(samples), 'blk', 0, 0)  43 us
  transfers between devices with their start and end apart: 7, of which 7 were waited for; matrix products, arithmetic and copies ran while one was open for 18% of the time, Pallas kernels for 0%

profile of v1, /device:TPU:32, one launch (start us, length us, event | category | flops | bytes accessed | tf_op | source)
XLA Modules:
  0.0 508.6 jit_solution(4291958274437056114)
XLA Ops:
  9.3 43.0 %all_to_all.5 = f32[4,2,128,512]{3,2,1,0:T(8,128)S(1)} all-to-all(f32[4,2,128,512]{3,2,1,0:T(8,128)S(1)} %stack.28), channel_id=1, replica_groups=mesh['tm_0'=8,'tm_1'=4,'tm_2'=2,'blk'=4] {'blk'}, dimensions={0} | all-to-all | bytes 4194304 | tf_op jit(solution)/shard_map/all_to_all | solution.py:50
  53.7 2.8 fusion.193
  56.8 4.4 fusion.142
  61.2 14.1 %all-gather.34.cloned.1.call-done = f32[1024,512]{1,0:T(8,128)} async-done(((f32[512,512]{1,0:T(8,128)}), f32[1024,512]{1,0:T(8,128)}) %all-gather.34.cloned.1.call-update) | async-done | bytes 2097168 | tf_op jit(solution)/shard_map/all_gather | solution.py:21
  78.6 4.0 fusion.84
  82.7 11.8 %all-gather.28.cloned.1.call-done = f32[1024,512]{1,0:T(8,128)} async-done(((f32[512,512]{1,0:T(8,128)}), f32[1024,512]{1,0:T(8,128)}) %all-gather.28.cloned.1.call-update) | async-done | bytes 2097168 | tf_op jit(solution)/shard_map/all_gather | solution.py:21
  97.6 4.1 fusion.136
  101.9 46.2 %all-gather.36.cloned.1.call-done = f32[2048,512]{1,0:T(8,128)} async-done(((f32[512,512]{1,0:T(8,128)}), f32[2048,512]{1,0:T(8,128)}) %all-gather.36.cloned.1.call-update) | async-done | bytes 4194320 | tf_op jit(solution)/shard_map/all_gather | solution.py:21
  151.5 3.1 fusion.69
  158.4 2.8 fusion.77
  161.5 39.4 %all-gather.30.cloned.1.call-done = f32[2048,512]{1,0:T(8,128)} async-done(((f32[512,512]{1,0:T(8,128)}), f32[2048,512]{1,0:T(8,128)}) %all-gather.30.cloned.1.call-update) | async-done | bytes 4194320 | tf_op jit(solution)/shard_map/all_gather | solution.py:21
  200.9 2.3 fusion.34
  204.3 3.1 fusion.121
  211.1 2.9 fusion.129
  214.5 9.9 %all_gather.88 = f32[2,512]{1,0:T(2,128)S(1)} all-gather(f32[2,128]{1,0:T(2,128)S(1)} %bitcast.353), channel_id=1, replica_groups=mesh['tm_0'=8,'tm_1'=4,'tm_2'=2,'blk'=4] {'blk'}, dimensions={1}, use_global_device_ids=true | all-gather | bytes 5120 | tf_op jit(solution)/shard_map/all_gather | solution.py:56
  236.2 10.4 %all-gather.13 = f32[4,1,512]{2,1,0:T(1,128)S(1)} all-gather(f32[1,1,512]{2,1,0:T(1,128)S(1)} %bitcast.338), channel_id=6, replica_groups=mesh['tm_0'=8,'tm_1'=4,'tm_2'=2,'blk'=4] {'tm_1'}, dimensions={0}, use_global_device_ids=true | all-gather | bytes 10240 | tf_op jit(solution)/shard_map/all_gather | solution.py:21
  248.2 2.4 fusion.67
  250.6 3.0 fusion.20
  257.6 23.5 %all-gather.14 = f32[8,1,512]{2,1,0:T(1,128)S(1)} all-gather(f32[1,1,512]{2,1,0:T(1,128)S(1)} %bitcast.348), channel_id=7, replica_groups=mesh['tm_0'=8,'tm_1'=4,'tm_2'=2,'blk'=4] {'tm_0'}, dimensions={0}, use_global_device_ids=true | all-gather | bytes 18432 | tf_op jit(solution)/shard_map/all_gather | solution.py:21
  282.1 3.0 fusion.6
  285.2 10.1 %all-gather.38.cloned.1.call-done = f32[4096,512]{1,0:T(8,128)} async-done(((f32[512,512]{1,0:T(8,128)}), f32[4096,512]{1,0:T(8,128)}) %all-gather.38.cloned.1.call-update) | async-done | bytes 8388624 | tf_op jit(solution)/shard_map/all_gather | solution.py:21
  295.3 2.3 fusion.37
  297.6 2.5 fusion.29
  300.2 3.1 fusion.39
  303.2 3.1 fusion.43
  319.0 71.0 %all-gather.32.cloned.1.call-done = f32[4096,512]{1,0:T(8,128)} async-done(((f32[512,512]{1,0:T(8,128)}), f32[4096,512]{1,0:T(8,128)}) %all-gather.32.cloned.1.call-update) | async-done | bytes 8388624 | tf_op jit(solution)/shard_map/all_gather | solution.py:21
  392.3 2.3 fusion.93
  394.7 2.5 fusion.97
  403.9 2.6 fusion.113
  429.6 9.7 %all_gather.101 = f32[2,512]{1,0:T(2,128)S(1)} all-gather(f32[2,128]{1,0:T(2,128)S(1)} %bitcast.352), channel_id=1, replica_groups=mesh['tm_0'=8,'tm_1'=4,'tm_2'=2,'blk'=4] {'blk'}, dimensions={1}, use_global_device_ids=true | all-gather | bytes 5120 | tf_op jit(solution)/shard_map/all_gather | solution.py:76
  443.2 11.3 %all-gather.16 = f32[4,1,512]{2,1,0:T(1,128)S(1)} all-gather(f32[1,1,512]{2,1,0:T(1,128)S(1)} %bitcast.337), channel_id=12, replica_groups=mesh['tm_0'=8,'tm_1'=4,'tm_2'=2,'blk'=4] {'tm_1'}, dimensions={0}, use_global_device_ids=true | all-gather | bytes 10240 | tf_op jit(solution)/shard_map/all_gather | solution.py:21
  458.6 23.3 %all-gather.17 = f32[8,1,512]{2,1,0:T(1,128)S(1)} all-gather(f32[1,1,512]{2,1,0:T(1,128)S(1)} %bitcast.344), channel_id=13, replica_groups=mesh['tm_0'=8,'tm_1'=4,'tm_2'=2,'blk'=4] {'tm_0'}, dimensions={0}, use_global_device_ids=true | all-gather | bytes 18432 | tf_op jit(solution)/shard_map/all_gather | solution.py:21
  (216 shorter events, 113.2 us)
Async XLA Ops:
  7.2 422.0 %copy-start = (f32[2,128,512]{2,1,0:T(8,128)S(1)}, f32[2,128,512]{2,1,0:T(8,128)}, u32[]{:S(2)}) copy-start(f32[2,128,512]{2,1,0:T(8,128)} %param.11) | copy-start | bytes 1572868
  7.2 49.6 %all-gather.26.cloned.1.call-start = ((), (), s32[]{:S(2)}) async-start(), calls=%async_computation.1 | async-start | bytes 2621440 | tf_op jit(solution)/shard_map/all_gather | solution.py:54
  7.9 67.5 %all-gather.34.cloned.1.call-start = ((), (), s32[]{:S(2)}) async-start(), calls=%async_computation.5 | async-start | bytes 3145728 | tf_op jit(solution)/shard_map/all_gather | solution.py:21
  56.6 37.9 %all-gather.28.cloned.1.call-start = ((), (), s32[]{:S(2)}) async-start(), calls=%async_computation.2 | async-start | bytes 3145728 | tf_op jit(solution)/shard_map/all_gather | solution.py:21
  61.2 86.9 %all-gather.36.cloned.1.call-start = ((), (), s32[]{:S(2)}) async-start(), calls=%async_computation.6 | async-start | bytes 5242880 | tf_op jit(solution)/shard_map/all_gather | solution.py:21
  82.6 118.3 %all-gather.30.cloned.1.call-start = ((), (), s32[]{:S(2)}) async-start(), calls=%async_computation.3 | async-start | bytes 5242880 | tf_op jit(solution)/shard_map/all_gather | solution.py:21
  101.7 193.6 %all-gather.38.cloned.1.call-start = ((), (), s32[]{:S(2)}) async-start(), calls=%async_computation.7 | async-start | bytes 9437184 | tf_op jit(solution)/shard_map/all_gather | solution.py:21
  161.3 228.8 %all-gather.32.cloned.1.call-start = ((), (), s32[]{:S(2)}) async-start(), calls=%async_computation.4 | async-start | bytes 9437184 | tf_op jit(solution)/shard_map/all_gather | solution.py:21
  208.3 18.2 %copy-start.3 = (f32[2,512,512]{2,1,0:T(8,128)S(1)}, f32[2,512,512]{2,1,0:T(8,128)}, u32[]{:S(2)}) copy-start(f32[2,512,512]{2,1,0:T(8,128)} %all-gather.26.cloned.1.call-done) | copy-start | bytes 6291460
  214.1 18.8 %copy-start.24 = (f32[512,512]{1,0:T(8,128)S(1)}, f32[512,512]{1,0:T(8,128)}, u32[]{:S(2)}) copy-start(f32[512,512]{1,0:T(8,128)} %copy-done.23) | copy-start | bytes 3145732
  214.1 18.8 %copy-start.25 = (f32[512,512]{1,0:T(8,128)S(1)}, f32[512,512]{1,0:T(8,128)}, u32[]{:S(2)}) copy-start(f32[512,512]{1,0:T(8,128)} %fusion.84) | copy-start | bytes 3145732
  214.1 20.0 %copy-start.38 = (f32[1024,512]{1,0:T(8,128)S(1)}, f32[1024,512]{1,0:T(8,128)}, u32[]{:S(2)}) copy-start(f32[1024,512]{1,0:T(8,128)} %all-gather.28.cloned.1.call-done) | copy-start | bytes 6291460
  226.5 20.5 %copy-start.17 = (f32[512,512]{1,0:T(8,128)S(1)}, f32[512,512]{1,0:T(8,128)}, u32[]{:S(2)}) copy-start(f32[512,512]{1,0:T(8,128)} %copy-done.16) | copy-start | bytes 3145732
  226.5 20.5 %copy-start.18 = (f32[512,512]{1,0:T(8,128)S(1)}, f32[512,512]{1,0:T(8,128)}, u32[]{:S(2)}) copy-start(f32[512,512]{1,0:T(8,128)} %fusion.136) | copy-start | bytes 3145732
  233.0 17.6 %copy-start.20 = (f32[512,512]{1,0:T(8,128)S(1)}, f32[512,512]{1,0:T(8,128)}, u32[]{:S(2)}) copy-start(f32[512,512]{1,0:T(8,128)} %copy-done.19) | copy-start | bytes 3145732
  233.0 17.6 %copy-start.22 = (f32[512,512]{1,0:T(8,128)S(1)}, f32[512,512]{1,0:T(8,128)}, u32[]{:S(2)}) copy-start(f32[512,512]{1,0:T(8,128)} %copy-done.21) | copy-start | bytes 3145732
  233.0 17.6 %copy-start.29 = (f32[512,512]{1,0:T(8,128)S(1)}, f32[512,512]{1,0:T(8,128)}, u32[]{:S(2)}) copy-start(f32[512,512]{1,0:T(8,128)} %fusion.77) | copy-start | bytes 3145732
  233.0 17.6 %copy-start.33 = (f32[512,512]{1,0:T(8,128)S(1)}, f32[512,512]{1,0:T(8,128)}, u32[]{:S(2)}) copy-start(f32[512,512]{1,0:T(8,128)} %copy-done.32) | copy-start | bytes 3145732
  234.2 19.4 %copy-start.35 = (f32[512,512]{1,0:T(8,128)}, f32[512,512]{1,0:T(8,128)S(1)}, u32[]{:S(2)}) copy-start(f32[512,512]{1,0:T(8,128)S(1)} %fusion.15) | copy-start | bytes 3145732
  253.5 28.5 %copy-start.13 = (f32[512,512]{1,0:T(8,128)S(1)}, f32[512,512]{1,0:T(8,128)}, u32[]{:S(2)}) copy-start(f32[512,512]{1,0:T(8,128)} %copy-done.12) | copy-start | bytes 3145732
  253.5 28.5 %copy-start.15 = (f32[512,512]{1,0:T(8,128)S(1)}, f32[512,512]{1,0:T(8,128)}, u32[]{:S(2)}) copy-start(f32[512,512]{1,0:T(8,128)} %copy-done.14) | copy-start | bytes 3145732
  253.5 28.5 %copy-start.28 = (f32[512,512]{1,0:T(8,128)S(1)}, f32[512,512]{1,0:T(8,128)}, u32[]{:S(2)}) copy-start(f32[512,512]{1,0:T(8,128)} %fusion.129) | copy-start | bytes 3145732
  253.6 28.5 %copy-start.31 = (f32[512,512]{1,0:T(8,128)S(1)}, f32[512,512]{1,0:T(8,128)}, u32[]{:S(2)}) copy-start(f32[512,512]{1,0:T(8,128)} %copy-done.30) | copy-start | bytes 3145732
  295.3 11.1 %copy-start.1 = (f32[4096,512]{1,0:T(8,128)S(1)}, f32[4096,512]{1,0:T(8,128)}, u32[]{:S(2)}) copy-start(f32[4096,512]{1,0:T(8,128)} %all-gather.38.cloned.1.call-done) | copy-start | bytes 25165828
  390.0 18.7 %copy-start.34 = (f32[512,512]{1,0:T(8,128)S(1)}, f32[512,512]{1,0:T(8,128)}, u32[]{:S(2)}) copy-start(f32[512,512]{1,0:T(8,128)} %fusion.6) | copy-start | bytes 3145732
  392.3 17.4 %copy-start.2 = (f32[4096,512]{1,0:T(8,128)S(1)}, f32[4096,512]{1,0:T(8,128)}, u32[]{:S(2)}) copy-start(f32[4096,512]{1,0:T(8,128)} %all-gather.32.cloned.1.call-done) | copy-start | bytes 25165828
  424.2 15.1 %copy-start.9 = (f32[1,4,128,512]{3,2,0,1:T(8,128)S(1)}, f32[1,4,128,512]{3,2,0,1:T(8,128)}, u32[]{:S(2)}) copy-start(f32[1,4,128,512]{3,2,0,1:T(8,128)} %copy-done.8) | copy-start | bytes 3145732
  424.2 18.0 %copy-start.37 = (f32[1024,512]{1,0:T(8,128)S(1)}, f32[1024,512]{1,0:T(8,128)}, u32[]{:S(2)}) copy-start(f32[1024,512]{1,0:T(8,128)} %all-gather.34.cloned.1.call-done) | copy-start | bytes 6291460
  424.3 30.3 %copy-start.5 = (f32[2048,512]{1,0:T(8,128)S(1)}, f32[2048,512]{1,0:T(8,128)}, u32[]{:S(2)}) copy-start(f32[2048,512]{1,0:T(8,128)} %all-gather.36.cloned.1.call-done) | copy-start | bytes 12582916
  427.1 30.5 %copy-start.36 = (f32[512,512]{1,0:T(8,128)S(1)}, f32[512,512]{1,0:T(8,128)}, u32[]{:S(2)}) copy-start(f32[512,512]{1,0:T(8,128)} %copy-done.35) | copy-start | bytes 3145732
  457.6 40.0 %copy-start.27 = (f32[512,512]{1,0:T(8,128)S(1)}, f32[512,512]{1,0:T(8,128)}, u32[]{:S(2)}) copy-start(f32[512,512]{1,0:T(8,128)} %fusion.20) | copy-start | bytes 3145732
  481.9 17.0 %copy-start.11 = (f32[1,4,128,512]{3,2,0,1:T(8,128)S(1)}, f32[1,4,128,512]{3,2,0,1:T(8,128)}, u32[]{:S(2)}) copy-start(f32[1,4,128,512]{3,2,0,1:T(8,128)} %copy-done.10) | copy-start | bytes 3145732
  (18 other events, 52.0 us)
Sparse Core Ops, SparseCore 0:
  9.8 46.9 all-gather.25
  58.6 16.7 all-gather.33
  77.2 17.1 all-gather.27
  96.1 52.0 all-gather.35
  149.8 51.0 all-gather.29
  202.6 92.6 all-gather.37
  297.1 92.9 all-gather.31
